TPU v7x, 32 devices: a whole 2x2x4 slice. The times are simulated.
32 devices in a mesh: tm: 16 (over z, y, x), state: 2 (over core).
Axes of the slice: x: 2, y: 2, z: 4, core: 2. Of those that a mesh axis runs over, the one named last changes fastest.
Arguments:
- symbols: int32 [8], P('state'), may hold values from 0 to 255
- emission: float32 [8192, 256], P('tm'), may hold values from 0.2 to 5
- decay: float32 [2, 8192], P('state', 'tm'), may hold values from 0.05 to 1
- left_factor: float32 [2, 64, 8192], P('state', None, 'tm'), may hold values from 0.1 to 3
- right_factor: float32 [2, 64, 8192], P('state', None, 'tm'), may hold values from 0.001 to 0.03
- initial: float32 [8192], P('tm'), may hold values from 0.1 to 10
Outputs:
- filtered: float32 [8, 8192], P('state', 'tm')
- log_scale: float32 [8], P('state')
All inputs are finite; a program needn't handle non-finite values.
Results may differ from a plain program's by a relative error of at most 0.00011.
Values sent between devices are 32-bit elements; how exact they have to be, the bound alone decides.
No kernel may reach another device: no remote copies, remote signals or barrier semaphores. Data moves between devices by JAX's collectives and lax.ppermute only.
A program may use at most 64 MiB of HBM per device.

v0:
```python
import jax
import jax.numpy as jnp
from jax import lax
from jax.sharding import PartitionSpec as P

S = 8192
PRECISE = lax.Precision.HIGHEST


def passed_along(value, axis, steps):
    count = lax.axis_size(axis)
    first, last = (max(0, -steps), min(count, count - steps))
    return lax.ppermute(value, axis, [(source, source + steps) for source in range(first, last)])


def run_span(entry_vec, emitted_all, decay_row, left_rows, right_rows):
    projected, total_sum = lax.psum(
        (jnp.dot(left_rows, entry_vec, precision=PRECISE), jnp.sum(entry_vec)), "tm"
    )
    rescale = S / total_sum
    belief = entry_vec * rescale
    mixture = projected * rescale / S

    def frame(state_pair, emitted):
        belief_now, mixture_now = state_pair
        unscaled = emitted * (
            decay_row * belief_now + jnp.dot(mixture_now, right_rows, precision=PRECISE)
        )
        proj_next, total_next = lax.psum(
            (jnp.dot(left_rows, unscaled, precision=PRECISE), jnp.sum(unscaled)), "tm"
        )
        normal = total_next / S
        belief_next = unscaled / normal
        mixture_next = proj_next / normal / S
        return ((belief_next, mixture_next), (belief_next, jnp.log(normal)))

    (closing, mixture_end), (beliefs, log_levels) = lax.scan(frame, (belief, mixture), emitted_all)
    return (beliefs, log_levels, closing)


def span_map(emitted_all, decay_row, left_rows, right_rows):
    frames = emitted_all.shape[0]
    rank_cols = left_rows.shape[0]
    cells = left_rows.shape[1]
    growth = emitted_all * decay_row[None, :]
    markers = jnp.eye(frames, dtype=jnp.float32)

    def advance(state_pair, inputs):
        reached, weights = state_pair
        grow_row, emitted, marker = inputs
        weights_next = weights * grow_row[None, :] + marker[:, None] * emitted[None, :]
        return ((reached * grow_row, weights_next), (reached, weights_next))

    begin_pair = (jnp.ones((cells,), jnp.float32), jnp.zeros((frames, cells), jnp.float32))
    (final_reach, final_weights), (reached_all, weights_all) = lax.scan(
        advance, begin_pair, (growth, emitted_all, markers)
    )
    probes = (left_rows[None, :, :] * reached_all[:, None, :]).reshape(
        frames * rank_cols, cells
    ) / S
    vb_rows = right_rows[None, :, :] * final_weights[:, None, :]
    pair_rows = weights_all[: frames - 1].reshape((frames - 1) * frames, cells)
    group_size = max(rank_cols // 8, 1)
    blocks = []
    for offset in range(0, rank_cols, group_size):
        cross_rows = (
            left_rows[offset : offset + group_size, None, :] * right_rows[None, :, :]
        ).reshape(-1, cells)
        blocks.append(jnp.einsum("pw,qw->pq", pair_rows, cross_rows, precision=PRECISE))
    local_terms = jnp.concatenate(blocks, axis=1) / S
    coupling = lax.psum(local_terms, "tm").reshape(frames - 1, frames, rank_cols, rank_cols)
    shifted = jnp.concatenate(
        [jnp.zeros((1, frames, rank_cols, rank_cols), jnp.float32), coupling], axis=0
    )

    def solve_back(turn_index, response):
        column = frames - 1 - turn_index
        factors = lax.dynamic_index_in_dim(shifted, column, 1, keepdims=False)
        coupled = jnp.einsum("kab,kaw->bw", factors, response, precision=PRECISE)
        own_rows = lax.dynamic_index_in_dim(vb_rows, column, 0, keepdims=False)
        return lax.dynamic_update_index_in_dim(response, own_rows + coupled, column, 0)

    response = lax.fori_loop(
        0, frames, solve_back, jnp.zeros((frames, rank_cols, cells), jnp.float32)
    )
    return (probes, final_reach, response)


def per_device(symbols, emission, decay, left_factor, right_factor, initial):
    decay_row = decay[0]
    left_rows = left_factor[0]
    right_rows = right_factor[0]
    onehot = (symbols[:, None] == jnp.arange(emission.shape[1], dtype=jnp.int32)[None, :]).astype(
        jnp.float32
    )
    emitted_all = jnp.einsum("fv,sv->fs", onehot, emission, precision=PRECISE)
    leader = lax.axis_index("state") == 0

    def pass_on(closing):
        return jnp.where(leader, initial, passed_along(closing, "state", 1))

    probes, final_reach, response = span_map(emitted_all, decay_row, left_rows, right_rows)
    frames = emitted_all.shape[0]
    rank_cols = left_rows.shape[0]

    def section(step_idx, entry_vec):
        projected, total_sum = lax.psum(
            (jnp.dot(probes, entry_vec, precision=PRECISE), jnp.sum(entry_vec)), "tm"
        )
        rescale = S / total_sum
        carried = jnp.einsum(
            "ka,kaw->w",
            (projected * rescale).reshape(frames, rank_cols),
            response,
            precision=PRECISE,
        )
        return pass_on(final_reach * entry_vec * rescale + carried)

    entry_vec = lax.fori_loop(0, lax.axis_size("state") - 1, section, initial)
    beliefs, log_levels, closing = run_span(
        entry_vec, emitted_all, decay_row, left_rows, right_rows
    )
    return (beliefs, log_levels)


def solution(mesh):
    return jax.shard_map(
        per_device,
        mesh=mesh,
        in_specs=(
            P("state"),
            P("tm", None),
            P("state", "tm"),
            P("state", None, "tm"),
            P("state", None, "tm"),
            P("tm"),
        ),
        out_specs=(P("state", "tm"), P("state")),
        check_vma=False,
    )
```

profile of v0, /device:TPU:0, one launch (start us, length us, event | category | flops | bytes accessed | tf_op | source)
XLA Modules:
  0.0 347.2 jit_solution(12387997942848952314)
XLA Ops:
  7.3 0.9 slice_bitcast_fusion
  8.3 0.6 copy-done.3
  8.9 0.4 broadcast_multiply_fusion.10
  9.3 0.8 while.54
  10.2 1.1 broadcast_multiply_fusion
  11.3 1.0 convolution_dynamic-update-slice_fusion.7
  12.2 1.0 convolution_dynamic-update-slice_fusion.6
  13.2 1.0 convolution_dynamic-update-slice_fusion.5
  14.2 1.0 convolution_dynamic-update-slice_fusion.4
  15.2 1.0 convolution_dynamic-update-slice_fusion.3
  16.1 1.0 convolution_dynamic-update-slice_fusion.2
  17.1 1.0 convolution_dynamic-update-slice_fusion.1
  18.1 1.0 convolution_dynamic-update-slice_fusion
  19.3 0.9 copy.8
  20.2 0.9 copy-done.1
  21.2 0.6 copy-done.4
  21.8 0.6 reduce_sum.28
  22.4 0.5 fusion.17
  22.9 44.2 %all-reduce.3 = (f32[256]{0:T(256)S(1)}, f32[]{:T(128)}) all-reduce(f32[256]{0:T(256)S(1)} %bitcast.161, f32[]{:T(128)} %reduce_sum.28), channel_id=1, replica_groups=mesh['tm'=16,'state'=2] {'tm'}, use_global_device_ids=true, to_apply=%region_4.5 | all-reduce | flops 257 | bytes 2056 | tf_op jit(solution)/shard_map/while/body/eval_jaxpr/psum | solution.py:107
  67.9 63.9 %all-reduce.8.cloned.1.call-done = f32[3,4,64,64]{2,3,0,1:T(8,128)} async-done(((f32[3,4,64,64]{2,3,0,1:T(8,128)}), f32[3,4,64,64]{2,3,0,1:T(8,128)}) %all-reduce.8.cloned.1.call-update) | async-done | bytes 196624 | tf_op jit(solution)/shard_map/psum | solution.py:71
  131.8 1.0 concatenate.7
  132.9 2.0 while.52
  133.0 0.5 fusion.58
  133.4 0.4 fusion.58
  133.9 0.5 fusion.58
  134.4 0.4 fusion.58
  134.9 0.4 fusion.18
  135.3 1.3 collective-permute-start
  136.6 0.8 collective-permute-done
  137.4 0.6 fusion.16
  138.0 0.2 convolution_bitcast_fusion.2
  138.2 40.5 %all-reduce.2 = (f32[]{:T(128)}, f32[64]{0:T(128)S(1)}) all-reduce(f32[]{:T(128)} %get-tuple-element.314, f32[64]{0:T(128)S(1)} %convolution_bitcast_fusion.2), channel_id=1, replica_groups=mesh['tm'=16,'state'=2] {'tm'}, use_global_device_ids=true, to_apply=%region_9.10 | all-reduce | flops 65 | bytes 520 | tf_op jit(solution)/shard_map/psum | solution.py:17
  179.4 160.4 %while.53 = (s32[]{:T(128)}, f32[512]{0:T(512)S(1)}, f32[64]{0:T(128)S(1)}, f32[4,512]{1,0:T(4,128)S(1)}, f32[4]{0:T(128)S(1)}, /*index=5*/f32[4,512]{1,0:T(4,12...) while((s32[]{:T(128)}, f32[512]{0:T(512)S(1)}, ...), condition=%wide.region_15.16_spmd, body=%wide.region_11.15_spmd.sunk | while | flops 789187 | bytes 290481 | solution.py:37
  179.4 0.2 fusion.63
  179.6 0.6 fusion.64
  180.2 0.2 convolution_bitcast_fusion.4
  180.4 37.2 %all-reduce.5 = (f32[]{:T(128)}, f32[64]{0:T(128)S(1)}) all-reduce(f32[]{:T(128)} %get-tuple-element.468, f32[64]{0:T(128)S(1)} %convolution_bitcast_fusion.4), channel_id=1, replica_groups=mesh['tm'=16,'state'=2] {'tm'}, use_global_device_ids=true, to_apply=%region_13.13 | all-reduce | flops 65 | bytes 520 | tf_op jit(solution)/shard_map/while/body/eval_jaxpr/psum | solution.py:29
  218.5 0.2 fusion.63
  218.7 0.6 fusion.64
  219.3 0.2 convolution_bitcast_fusion.4
  219.5 39.2 %all-reduce.5 = (f32[]{:T(128)}, f32[64]{0:T(128)S(1)}) all-reduce(f32[]{:T(128)} %get-tuple-element.468, f32[64]{0:T(128)S(1)} %convolution_bitcast_fusion.4), channel_id=1, replica_groups=mesh['tm'=16,'state'=2] {'tm'}, use_global_device_ids=true, to_apply=%region_13.13 | all-reduce | flops 65 | bytes 520 | tf_op jit(solution)/shard_map/while/body/eval_jaxpr/psum | solution.py:29
  259.6 0.2 fusion.63
  259.8 0.6 fusion.64
  260.5 37.3 %all-reduce.5 = (f32[]{:T(128)}, f32[64]{0:T(128)S(1)}) all-reduce(f32[]{:T(128)} %get-tuple-element.468, f32[64]{0:T(128)S(1)} %convolution_bitcast_fusion.4), channel_id=1, replica_groups=mesh['tm'=16,'state'=2] {'tm'}, use_global_device_ids=true, to_apply=%region_13.13 | all-reduce | flops 65 | bytes 520 | tf_op jit(solution)/shard_map/while/body/eval_jaxpr/psum | solution.py:29
  298.7 0.2 fusion.63
  298.9 0.6 fusion.64
  299.7 39.2 %all-reduce.5 = (f32[]{:T(128)}, f32[64]{0:T(128)S(1)}) all-reduce(f32[]{:T(128)} %get-tuple-element.468, f32[64]{0:T(128)S(1)} %convolution_bitcast_fusion.4), channel_id=1, replica_groups=mesh['tm'=16,'state'=2] {'tm'}, use_global_device_ids=true, to_apply=%region_13.13 | all-reduce | flops 65 | bytes 520 | tf_op jit(solution)/shard_map/while/body/eval_jaxpr/psum | solution.py:29
  339.8 0.5 copy-done.7
  (79 shorter events, 2.6 us)
Async XLA Ops:
  7.2 1.2 copy-start
  7.2 124.7 %all-reduce.8.cloned.1.call-start = ((), (), s32[]{:S(2)}) async-start(), calls=%async_computation | async-start | bytes 786432 | tf_op jit(solution)/shard_map/psum | solution.py:71
  8.2 0.7 copy-start.3
  8.2 0.7 copy-start.6
  9.2 0.9 copy-start.2
  20.2 0.9 copy-start.1
  21.1 0.7 copy-start.4
  135.3 2.1 collective-permute-start
  339.8 0.5 copy-start.7
  339.8 0.6 copy-start.5
Sparse Core Ops, SparseCore 0:
  20.3 111.4 all-reduce.7
where the time goes:
time: 348 us; the launch traced here: 347 us
  blocking collectives  238 us (68%)
  waiting for transfers between devices  64.7 us (19%)
  between operations  15.6 us (4%)
  matrix products  12.4 us (4%)
  local copies, waits for them, and re-layouts  7.07 us (2%)
  other arithmetic  5.31 us (2%)
    psum x4, blocking collectives, frame(): lax.psum((jnp.dot(left_rows, unscaled, precision=PRECISE), jnp.sum(unscal...  153 us
    psum x1, waiting for transfers between devices, span_map(): lax.psum(local_terms, 'tm')  63.9 us
    psum x1, blocking collectives, section(): lax.psum((jnp.dot(probes, entry_vec, precision=PRECISE), jnp.sum(entry_ve...  44.2 us
    psum x1, blocking collectives, run_span(): lax.psum((jnp.dot(left_rows, entry_vec, precision=PRECISE), jnp.sum(entry...  40.5 us
    dot_general x8, matrix products, span_map(): jnp.einsum('pw,qw->pq', pair_rows, cross_rows, precision=PRECISE)  7.79 us
  transfers between devices with their start and end apart: 2, of which 2 were waited for; matrix products, arithmetic and copies ran while one was open for 0% of the time, Pallas kernels for 0%

commit v1 on v0

--- a/solution.py
+++ b/solution.py
@@ -68,7 +68,9 @@
         ).reshape(-1, cells)
         blocks.append(jnp.einsum("pw,qw->pq", pair_rows, cross_rows, precision=PRECISE))
     local_terms = jnp.concatenate(blocks, axis=1) / S
-    coupling = lax.psum(local_terms, "tm").reshape(frames - 1, frames, rank_cols, rank_cols)
+    coupling = jnp.sum(lax.all_gather(local_terms, "tm"), axis=0).reshape(
+        frames - 1, frames, rank_cols, rank_cols
+    )
     shifted = jnp.concatenate(
         [jnp.zeros((1, frames, rank_cols, rank_cols), jnp.float32), coupling], axis=0
     )

time: 348 us -> 316 us (0.908)
  waiting for transfers between devices: 64.7 us -> 32.9 us
  other arithmetic: 5.31 us -> 9.34 us
  local copies, waits for them, and re-layouts: 7.07 us -> 3.04 us
    psum x1 -> x0, waiting for transfers between devices: 63.9 us -> none  [span_map(): lax.psum(local_terms, 'tm')]
    all_gather x0 -> x1, waiting for transfers between devices: none -> 32.1 us  [span_map(): lax.all_gather(local_terms, 'tm')]
where the time goes in v1:
time: 316 us
  blocking collectives  237 us (75%)
  waiting for transfers between devices  32.9 us (10%)
  between operations  15.6 us (5%)
  matrix products  12.9 us (4%)
  other arithmetic  9.34 us (3%)
  loops' own time  3.19 us (1%)
    psum x4, blocking collectives, frame(): lax.psum((jnp.dot(left_rows, unscaled, precision=PRECISE), jnp.sum(unscal...  153 us
    psum x1, blocking collectives, section(): lax.psum((jnp.dot(probes, entry_vec, precision=PRECISE), jnp.sum(entry_ve...  44.4 us
    psum x1, blocking collectives, run_span(): lax.psum((jnp.dot(left_rows, entry_vec, precision=PRECISE), jnp.sum(entry...  40.1 us
    all_gather x1, waiting for transfers between devices, span_map(): lax.all_gather(local_terms, 'tm')  32.1 us
    dot_general x8, matrix products, span_map(): jnp.einsum('pw,qw->pq', pair_rows, cross_rows, precision=PRECISE)  7.78 us
  transfers between devices with their start and end apart: 2, of which 2 were waited for; matrix products, arithmetic and copies ran while one was open for 0% of the time, Pallas kernels for 0%

profile of v1, /device:TPU:0, one launch (start us, length us, event | category | flops | bytes accessed | tf_op | source)
XLA Modules:
  0.0 315.7 jit_solution(13033362899725686888)
XLA Ops:
  7.3 0.9 slice_bitcast_fusion
  8.2 0.2 copy-done
  8.3 1.0 broadcast_multiply_fusion.10
  9.4 0.8 while.54
  10.2 2.0 broadcast_multiply_fusion
  12.2 1.0 fusion.16
  13.2 1.0 fusion.15
  14.2 1.0 fusion.14
  15.2 1.0 fusion.13
  16.1 1.0 fusion.12
  17.1 1.0 fusion.11
  18.1 1.0 fusion.10
  19.1 1.0 fusion.9
  20.0 0.7 broadcast_multiply_fusion.9
  20.8 0.6 reduce_sum.37
  21.5 0.5 fusion.25
  22.0 44.4 %all-reduce.3 = (f32[256]{0:T(256)S(1)}, f32[]{:T(128)}) all-reduce(f32[256]{0:T(256)S(1)} %bitcast.194, f32[]{:T(128)} %reduce_sum.37), channel_id=1, replica_groups=mesh['tm'=16,'state'=2] {'tm'}, use_global_device_ids=true, to_apply=%region_4.5 | all-reduce | flops 257 | bytes 2056 | tf_op jit(solution)/shard_map/while/body/eval_jaxpr/psum | solution.py:109
  67.2 32.1 %all-gather.2.cloned.1.call-done = f32[16,12,4096]{2,1,0:T(8,128)} async-done(((f32[1,12,4096]{2,1,0:T(8,128)}), f32[16,12,4096]{2,1,0:T(8,128)}) %all-gather.2.cloned.1.call-update) | async-done | bytes 3145744 | tf_op jit(solution)/shard_map/all_gather | solution.py:71
  99.2 2.4 reduce_sum.38
  102.0 1.8 while.52
  102.0 0.4 fusion.66
  102.4 0.4 fusion.66
  102.9 0.4 fusion.66
  103.3 0.4 fusion.66
  103.8 0.4 fusion.26
  104.1 1.3 collective-permute-start
  105.5 0.8 collective-permute-done
  106.2 0.6 fusion.24
  106.8 0.2 convolution_bitcast_fusion.10
  107.0 40.1 %all-reduce.2 = (f32[]{:T(128)}, f32[64]{0:T(128)S(1)}) all-reduce(f32[]{:T(128)} %get-tuple-element.322, f32[64]{0:T(128)S(1)} %convolution_bitcast_fusion.10), channel_id=1, replica_groups=mesh['tm'=16,'state'=2] {'tm'}, use_global_device_ids=true, to_apply=%region_9.10 | all-reduce | flops 65 | bytes 520 | tf_op jit(solution)/shard_map/psum | solution.py:17
  147.8 160.4 %while.53 = (s32[]{:T(128)}, f32[512]{0:T(512)S(1)}, f32[64]{0:T(128)S(1)}, f32[4,512]{1,0:T(4,128)S(1)}, f32[4]{0:T(128)S(1)}, /*index=5*/f32[4,512]{1,0:T(4,12...) while((s32[]{:T(128)}, f32[512]{0:T(512)S(1)}, ...), condition=%wide.region_15.16_spmd, body=%wide.region_11.15_spmd.sunk | while | flops 789187 | bytes 290481 | solution.py:37
  147.8 0.2 fusion.71
  148.0 0.6 fusion.72
  148.6 0.2 convolution_bitcast_fusion.12
  148.8 37.2 %all-reduce.5 = (f32[]{:T(128)}, f32[64]{0:T(128)S(1)}) all-reduce(f32[]{:T(128)} %get-tuple-element.478, f32[64]{0:T(128)S(1)} %convolution_bitcast_fusion.12), channel_id=1, replica_groups=mesh['tm'=16,'state'=2] {'tm'}, use_global_device_ids=true, to_apply=%region_13.13 | all-reduce | flops 65 | bytes 520 | tf_op jit(solution)/shard_map/while/body/eval_jaxpr/psum | solution.py:29
  186.9 0.2 fusion.71
  187.1 0.6 fusion.72
  187.7 0.2 convolution_bitcast_fusion.12
  187.9 39.2 %all-reduce.5 = (f32[]{:T(128)}, f32[64]{0:T(128)S(1)}) all-reduce(f32[]{:T(128)} %get-tuple-element.478, f32[64]{0:T(128)S(1)} %convolution_bitcast_fusion.12), channel_id=1, replica_groups=mesh['tm'=16,'state'=2] {'tm'}, use_global_device_ids=true, to_apply=%region_13.13 | all-reduce | flops 65 | bytes 520 | tf_op jit(solution)/shard_map/while/body/eval_jaxpr/psum | solution.py:29
  228.0 0.2 fusion.71
  228.2 0.6 fusion.72
  228.8 0.2 convolution_bitcast_fusion.12
  229.0 37.3 %all-reduce.5 = (f32[]{:T(128)}, f32[64]{0:T(128)S(1)}) all-reduce(f32[]{:T(128)} %get-tuple-element.478, f32[64]{0:T(128)S(1)} %convolution_bitcast_fusion.12), channel_id=1, replica_groups=mesh['tm'=16,'state'=2] {'tm'}, use_global_device_ids=true, to_apply=%region_13.13 | all-reduce | flops 65 | bytes 520 | tf_op jit(solution)/shard_map/while/body/eval_jaxpr/psum | solution.py:29
  267.1 0.2 fusion.71
  267.3 0.6 fusion.72
  267.9 0.2 convolution_bitcast_fusion.12
  268.1 39.2 %all-reduce.5 = (f32[]{:T(128)}, f32[64]{0:T(128)S(1)}) all-reduce(f32[]{:T(128)} %get-tuple-element.478, f32[64]{0:T(128)S(1)} %convolution_bitcast_fusion.12), channel_id=1, replica_groups=mesh['tm'=16,'state'=2] {'tm'}, use_global_device_ids=true, to_apply=%region_13.13 | all-reduce | flops 65 | bytes 520 | tf_op jit(solution)/shard_map/while/body/eval_jaxpr/psum | solution.py:29
  308.2 0.6 copy-done.5
  (76 shorter events, 2.0 us)
Async XLA Ops:
  7.2 1.2 copy-start
  7.2 92.1 %all-gather.2.cloned.1.call-start = ((), (), s32[]{:S(2)}) async-start(), calls=%async_computation | async-start | bytes 4456448 | tf_op jit(solution)/shard_map/all_gather | solution.py:71
  13.2 7.6 %copy-start.4 = (f32[512]{0:T(512)S(1)}, f32[512]{0:T(512)}, u32[]{:S(2)}) copy-start(f32[512]{0:T(512)} %param.17) | copy-start | bytes 6148
  13.2 8.2 %copy-start.1 = (f32[1,64,512]{2,1,0:T(8,128)S(1)}, f32[1,64,512]{2,1,0:T(8,128)}, u32[]{:S(2)}) copy-start(f32[1,64,512]{2,1,0:T(8,128)} %param.15) | copy-start | bytes 393220
  13.2 8.2 %copy-start.2 = (f32[1,64,512]{2,1,0:T(8,128)S(1)}, f32[1,64,512]{2,1,0:T(8,128)}, u32[]{:S(2)}) copy-start(f32[1,64,512]{2,1,0:T(8,128)} %param.16) | copy-start | bytes 393220
  101.8 46.0 %copy-start.3 = (f32[1,512]{1,0:T(1,128)S(1)}, f32[1,512]{1,0:T(1,128)}, u32[]{:S(2)}) copy-start(f32[1,512]{1,0:T(1,128)} %param.14) | copy-start | bytes 6148
  104.1 2.1 collective-permute-start
  308.2 0.6 copy-start.5
  308.2 0.6 copy-start.6
Sparse Core Ops, SparseCore 0:
  20.9 78.2 all-gather.1
